TPU v7x, 32 devices: a whole 2x2x4 slice. The times are simulated.
32 devices in a mesh: rep: 4 (over x, core), mx: 2 (over y), my: 4 (over z).
Axes of the slice: x: 2, y: 2, z: 4, core: 2. Of those that a mesh axis runs over, the one named last changes fastest.
Arguments:
- coefficients: bfloat16 [2, 384, 384, 384], P(None, 'mx', 'my'), may hold values from -7.5 to 7.5
- noise_field: bfloat16 [128, 2, 1536, 1536], P(('rep', 'mx'), None, 'my'), may hold values from -96 to 96
- mode_table: bfloat16 [384, 1536], replicated, may hold values from -0.3125 to 0.3125
Outputs:
- update: bfloat16 [2, 384, 384, 384], P(None, 'mx', 'my', 'rep')
All inputs are finite; a program needn't handle non-finite values.
Results may differ from a plain program's by a relative error of at most 0.008.
Values may be sent and summed in bfloat16 or wider, within the bound.
A program may use at most 384 MiB of HBM per device.

v0:
```python
import jax
import jax.numpy as jnp
from jax import lax
from jax.sharding import PartitionSpec as P

DAMPING = 0.25


def body(coefficients, noise_field, mode_table):
    rep_index = lax.axis_index("rep")
    col_index = lax.axis_index("my")
    rep_count = lax.axis_size("rep")
    row_count = lax.axis_size("mx")
    col_count = lax.axis_size("my")
    planes_dev = noise_field.shape[0]
    planes_rep = planes_dev * row_count
    planes_all = planes_rep * rep_count
    mode_count = mode_table.shape[0]
    point_count = mode_table.shape[1]
    slab_first = point_count // 2 - planes_all // 2
    row_block = mode_count // row_count
    col_block = mode_count // col_count
    point_block = point_count // col_count
    own_block = mode_count // rep_count
    slab_own = lax.dynamic_slice_in_dim(
        mode_table, slab_first + rep_index * planes_rep, planes_rep, 1
    )
    zmodes = jnp.einsum(
        "pabk,kz->zpba", coefficients, slab_own, preferred_element_type=jnp.float32
    ).astype(jnp.bfloat16)
    zmodes = zmodes.reshape(planes_rep, 2, col_block * row_block)
    spread = lax.all_to_all(zmodes, "mx", split_axis=0, concat_axis=2, tiled=True)
    grouped = spread.reshape(planes_dev, 2, row_count, col_block, row_block)
    tiled_table = mode_table.reshape(row_count, row_block, point_count)
    own_points = lax.dynamic_slice_in_dim(tiled_table, col_index * point_block, point_block, 2)
    block_part = jnp.einsum(
        "zpsal,slx->zpax",
        lax.all_gather(grouped, "my", axis=3, tiled=True),
        own_points,
        preferred_element_type=jnp.float32,
    ).astype(jnp.bfloat16)
    wave_field = jnp.einsum(
        "zpax,ay->zpxy", block_part, mode_table, preferred_element_type=jnp.float32
    )
    wave_real = wave_field[:, 0]
    wave_imag = wave_field[:, 1]
    density = wave_real * wave_real + wave_imag * wave_imag
    noise_wide = noise_field.astype(jnp.float32)
    drive_term = jnp.stack(
        [
            density * (wave_imag - DAMPING * wave_real) + noise_wide[:, 0],
            density * (-wave_real - DAMPING * wave_imag) + noise_wide[:, 1],
        ],
        1,
    ).astype(jnp.bfloat16)
    proj_columns = jnp.einsum(
        "zpxy,ny->zpnx", drive_term, mode_table, preferred_element_type=jnp.float32
    ).astype(jnp.bfloat16)
    block_part = lax.all_to_all(proj_columns, "my", split_axis=2, concat_axis=3, tiled=True)
    folded = jnp.einsum(
        "zpax,slx->zpsal", block_part, tiled_table, preferred_element_type=jnp.float32
    ).astype(jnp.bfloat16)
    proj_rows = folded.reshape(
        block_part.shape[0], block_part.shape[1], row_count * col_block * row_block
    )
    gathered_rows = lax.all_to_all(proj_rows, "mx", split_axis=2, concat_axis=0, tiled=True)
    slab_back = lax.dynamic_slice_in_dim(mode_table, rep_index * own_block, own_block, 0)[
        :, slab_first : slab_first + planes_all
    ]
    portion = lax.all_gather(gathered_rows, "rep", axis=0, tiled=True)
    plane_grid = portion.reshape(portion.shape[0], 2, col_block, row_block)
    summed = jnp.einsum("zpba,nz->pabn", plane_grid, slab_back, preferred_element_type=jnp.float32)
    return summed.astype(jnp.bfloat16)


def solution(mesh):
    in_specs = (P(None, "mx", "my", None), P(("rep", "mx"), None, "my", None), P())
    out_specs = P(None, "mx", "my", "rep")
    return jax.shard_map(body, mesh=mesh, in_specs=in_specs, out_specs=out_specs, check_vma=False)
```

profile of v0, /device:TPU:0, one launch (start us, length us, event | category | flops | bytes accessed | tf_op | source)
XLA Modules:
  0.0 974.2 jit_solution(4171945368356783076)
XLA Ops:
  6.5 0.0 copy-start
  6.5 0.0 all-gather.3.cloned.1.call-start
  6.5 1.3 copy-done
  7.8 25.5 %convert_bitcast_fusion.3 = bf16[32,2,96,192]{2,0,3,1:T(8,128)(2,1)} fusion(bf16[2,192,96,384]{3,2,1,0:T(8,128)(2,1)} %param.3, bf16[384,1536]{1,0:T(8,128)(2,1)S(1)} %copy-done, s32[]{:T(128)S(6)} %select_n.10), kind=kOutput, calls=%fused_computation.17 | convolution fusion | flops 907149312 | bytes 30769156 | tf_op jit(solution)/shard_map/pabk,kz->zpba/dot_general | solution.py:28
  33.3 5.1 copy.45
  38.5 6.9 reshape.28
  45.3 31.8 %all_to_all.51 = bf16[32,2,18432]{2,1,0:T(2,128)(2,1)S(1)} all-to-all(bf16[32,2,18432]{2,1,0:T(2,128)(2,1)S(1)} %reshape.28), channel_id=1, replica_groups=mesh['rep'=4,'mx'=2,'my'=4] {'mx'}, dimensions={0} | all-to-all | bytes 4718592 | tf_op jit(solution)/shard_map/all_to_all | solution.py:32
  77.1 2.4 copy.52
  79.5 4.5 reshape.17
  84.0 0.0 all-gather.3.cloned.1.call-update
  84.0 0.2 all-gather.5.cloned.1.call-start
  84.2 37.8 %convert_element_type.34 = f32[16,2,384,1536]{3,2,1,0:T(8,128)} convert(bf16[16,2,384,1536]{3,2,1,0:T(8,128)(2,1)} %param.4) | non-fusion elementwise | flops 18874368 | bytes 113246208 | tf_op jit(solution)/shard_map/convert_element_type | solution.py:48
  122.1 180.8 %all-gather.3.cloned.1.call-done = bf16[16,2,2,384,192]{4,3,2,1,0:T(8,128)(2,1)} async-done(((bf16[16,2,2,96,192]{4,3,2,1,0:T(8,128)(2,1)}), bf16[16,2,2,384,192]{4,3,2,1,0:T(8,128)(2,1)}) %all-gather.3.cloned.1.call-update) | async-done | bytes 9437200 | tf_op jit(solution)/shard_map/all_gather | solution.py:38
  302.9 36.1 %fusion.6 = f32[16,2,384,1536]{3,2,1,0:T(8,128)} fusion(bf16[16,2,2,384,192]{4,3,2,1,0:T(8,128)(2,1)} %all-gather.3.cloned.1.call-done, bf16[384,1536]{1,0:T(8,128)(2,1)S(1)} %copy-done, bf16[2,192,1536]{2,1,0:T(8,128)(2,1)S(1)} %bitcast.69, s32[]{:T(128)S(6)} %select_n.11), kind=kOutput, calls=%fused_computation.10 | convolution fusion | flops 18124111872 | bytes 86409216 | tf_op jit(solution)/shard_map/zpax,ay->zpxy/dot_general | solution.py:42
  339.0 61.5 %fusion.1 = (bf16[16,1,384,1536]{3,2,1,0:T(8,128)(2,1)}, bf16[16,1,384,1536]{3,2,1,0:T(8,128)(2,1)}) fusion(f32[16,2,384,1536]{3,2,1,0:T(8,128)} %convert_element_type.34, f32[16,2,384,1536]{3,2,1,0:T(8,128)} %fusion.6), kind=kLoop, calls=%fused_computation.3 | loop fusion | flops 132120576 | bytes 188743680 | tf_op jit(solution)/shard_map/convert
  400.5 26.7 %convert_bitcast_fusion.1 = bf16[16,2,384,384]{2,3,1,0:T(8,128)(2,1)} fusion(bf16[16,1,384,1536]{3,2,1,0:T(8,128)(2,1)} %get-tuple-element.6, bf16[16,1,384,1536]{3,2,1,0:T(8,128)(2,1)} %get-tuple-element.5, bf16[384,1536]{1,0:T(8,128)(2,1)S(1)} %copy-done), kind=kOutput, calls=%fused_computation.15 | convolution fusion | flops 14519107584 | bytes 48365568 | tf_op jit(solution)/shard_map/zpxy,ny->zpnx/dot_general | solution.py:56
  427.2 23.9 %copy.29 = bf16[16,2,384,384]{3,1,0,2:T(2,128)(2,1)} copy(bf16[16,2,384,384]{2,3,1,0:T(8,128)(2,1)} %convert_bitcast_fusion.1) | data formatting | bytes 18874368 | tf_op jit(solution)/shard_map/convert_element_type | solution.py:58
  451.1 214.1 %all_to_all.52 = bf16[16,2,384,384]{3,1,0,2:T(2,128)(2,1)} all-to-all(bf16[16,2,384,384]{3,1,0,2:T(2,128)(2,1)} %copy.29), channel_id=1, replica_groups=mesh['rep'=4,'mx'=2,'my'=4] {'my'}, dimensions={2} | all-to-all | bytes 18874368 | tf_op jit(solution)/shard_map/all_to_all | solution.py:59
  665.3 10.9 %copy.30 = bf16[16,2,384,384]{3,2,1,0:T(8,128)(2,1)} copy(bf16[16,2,384,384]{3,1,0,2:T(2,128)(2,1)} %all_to_all.52) | data formatting | bytes 18874368 | tf_op jit(solution)/shard_map/all_to_all | solution.py:59
  676.2 10.6 %copy.31 = bf16[16,2,96,4,384]{4,3,2,1,0:T(4,128)(2,1)} copy(bf16[16,2,96,4,384]{4,2,3,1,0:T(8,128)(2,1)} %bitcast.73) | data formatting | bytes 18874368 | tf_op jit(solution)/shard_map/all_to_all | solution.py:59
  686.8 15.9 %reshape.25 = bf16[16,2,96,1536,1]{3,2,1,0,4:T(8,128)(2,1)} reshape(bf16[16,2,96,4,384]{4,3,2,1,0:T(4,128)(2,1)} %copy.31) | data formatting | bytes 18874368 | tf_op jit(solution)/shard_map/all_to_all | solution.py:59
  702.7 10.2 %convert_bitcast_fusion.2 = bf16[16,2,2,96,192]{4,3,2,1,0:T(8,128)(2,1)} fusion(bf16[2,192,1536,1,1]{2,1,0,4,3:T(8,128)(2,1)S(1)} %bitcast.68, bf16[16,2,96,1536,1]{3,2,1,0,4:T(8,128)(2,1)} %reshape.25), kind=kOutput, calls=%fused_computation.16 | convolution fusion | flops 3625058304 | bytes 12976128 | tf_op jit(solution)/shard_map/zpax,slx->zpsal/dot_general | solution.py:60
  712.8 35.2 %copy.46 = bf16[16,2,2,96,192]{0,1,4,3,2:T(2,128)(2,1)} copy(bf16[16,2,2,96,192]{4,3,2,1,0:T(8,128)(2,1)} %convert_bitcast_fusion.2) | data formatting | bytes 4718592 | tf_op jit(solution)/shard_map/reshape | solution.py:63
  748.1 27.3 %reshape.30 = bf16[2,2,294912]{2,1,0:T(2,128)(2,1)S(1)} reshape(bf16[36864,2,16]{2,1,0:T(2,128)(2,1)} %bitcast.70) | data formatting | bytes 4718592
  775.3 30.9 %all_to_all.53 = bf16[2,2,294912]{2,1,0:T(2,128)(2,1)} all-to-all(bf16[2,2,294912]{2,1,0:T(2,128)(2,1)S(1)} %reshape.30), channel_id=1, replica_groups=mesh['rep'=4,'mx'=2,'my'=4] {'mx'}, dimensions={0} | all-to-all | bytes 4718592 | tf_op jit(solution)/shard_map/all_to_all | solution.py:66
  806.2 22.4 %reshape.31 = bf16[36864,2,16]{2,1,0:T(2,128)(2,1)} reshape(bf16[2,2,294912]{2,1,0:T(2,128)(2,1)} %all_to_all.53) | data formatting | bytes 4718592
  828.6 35.6 %copy.34 = bf16[2,16,2,18432]{3,1,0,2:T(8,128)(2,1)} copy(bf16[2,16,2,18432]{1,2,3,0:T(2,128)(2,1)} %bitcast.71) | data formatting | bytes 4718592 | tf_op jit(solution)/shard_map/all_to_all | solution.py:66
  864.2 0.0 all-gather.5.cloned.1.call-update
  864.2 62.8 %all-gather.5.cloned.1.call-done = bf16[128,2,18432]{2,0,1:T(8,128)(2,1)} async-done(((bf16[32,2,18432]{2,0,1:T(8,128)(2,1)}), bf16[128,2,18432]{2,0,1:T(8,128)(2,1)}) %all-gather.5.cloned.1.call-update) | async-done | bytes 9437200 | tf_op jit(solution)/shard_map/all_gather | solution.py:70
  927.0 12.6 %copy.35 = bf16[128,2,18432]{0,2,1:T(8,128)(2,1)} copy(bf16[128,2,18432]{2,0,1:T(8,128)(2,1)} %all-gather.5.cloned.1.call-done) | data formatting | bytes 18874368 | tf_op jit(solution)/shard_map/all_gather | solution.py:70
  939.6 13.8 %convert_bitcast_fusion = bf16[2,192,96,96]{1,3,2,0:T(8,128)(2,1)} fusion(bf16[128,2,96,192]{0,3,2,1:T(8,128)(2,1)} %bitcast.72, bf16[384,1536]{1,0:T(8,128)(2,1)S(1)} %copy-done, s32[]{:T(128)S(6)} %select_n.9, s32[]{:T(128)S(6)} %add.30), kind=kOutput, calls=%fused_computation.14 | convolution fusion | flops 909508608 | bytes 16539656 | tf_op jit(solution)/shard_map/zpba,nz->pabn/dot_general | solution.py:72
  953.3 13.9 %copy.36 = bf16[2,192,96,96]{3,2,1,0:T(8,128)(2,1)} copy(bf16[2,192,96,96]{1,3,2,0:T(8,128)(2,1)} %convert_bitcast_fusion) | data formatting | bytes 14155776 | tf_op jit(solution)/shard_map/convert_element_type | solution.py:73
Async XLA Ops:
  6.5 1.3 copy-start
  6.5 296.3 %all-gather.3.cloned.1.call-start = ((), (), s32[]{:S(2)}) async-start(), calls=%async_computation.3 | async-start | bytes 15728640 | tf_op jit(solution)/shard_map/all_gather | solution.py:38
  84.0 843.0 %all-gather.5.cloned.1.call-start = ((), (), s32[]{:S(2)}) async-start(), calls=%async_computation.4 | async-start | bytes 11796480 | tf_op jit(solution)/shard_map/all_gather | solution.py:70
Sparse Core Ops, SparseCore 0:
  84.1 218.6 all-gather.2
  864.3 62.6 all-gather.4
where the time goes:
time: 986 us; the launch traced here: 974 us
  blocking collectives  277 us (28%)
  waiting for transfers between devices  244 us (25%)
  local copies, waits for them, and re-layouts  228 us (23%)
  matrix products  112 us (11%)
  other arithmetic  99.4 us (10%)
  between operations  13.6 us (1%)
    all_to_all x1, blocking collectives, body(): lax.all_to_all(proj_columns, 'my', split_axis=2, concat_axis=3, tiled=True)  214 us
    all_gather x1, waiting for transfers between devices, body(): lax.all_gather(grouped, 'my', axis=3, tiled=True)  181 us
    all_gather x1, waiting for transfers between devices, body(): portion = lax.all_gather(gathered_rows, 'rep', axis=0, tiled=True)  62.8 us
    another operation x1, other arithmetic  61.5 us
    unnamed x4, local copies, waits for them, and re-layouts  50.9 us
    convert_element_type x1, other arithmetic, body(): noise_wide = noise_field.astype(jnp.float32)  37.8 us
    all_to_all x3, local copies, waits for them, and re-layouts, body(): lax.all_to_all(proj_columns, 'my', split_axis=2, concat_axis=3, tiled=True)  37.4 us
    dot_general x1, matrix products, body(): jnp.einsum('zpax,ay->zpxy', block_part, mode_table, preferred_element_typ...  36.1 us
  transfers between devices with their start and end apart: 2, of which 2 were waited for; matrix products, arithmetic and copies ran while one was open for 4% of the time, Pallas kernels for 0%

commit v1 on v0

--- a/solution.py
+++ b/solution.py
@@ -35,7 +35,7 @@
     own_points = lax.dynamic_slice_in_dim(tiled_table, col_index * point_block, point_block, 2)
     block_part = jnp.einsum(
         "zpsal,slx->zpax",
-        lax.all_gather(grouped, "my", axis=3, tiled=True),
+        jnp.concatenate(lax.all_gather(grouped, "my"), axis=3),
         own_points,
         preferred_element_type=jnp.float32,
     ).astype(jnp.bfloat16)

time: 986 us -> 1040 us (1.055)
  local copies, waits for them, and re-layouts: 228 us -> 274 us
    reshape x1 -> x2, local copies, waits for them, and re-layouts: 4.46 us -> 43.8 us  [body(): jnp.concatenate(lax.all_gather(grouped, 'my'), axis=3)]
    dot_general x0 -> x1, matrix products: none -> 10.7 us  [body(): jnp.einsum('zpsal,slx->zpax', jnp.concatenate(lax.all_gather(grouped, 'my...]
where the time goes in v1:
time: 1040 us; the launch traced here: 1030 us
  blocking collectives  277 us (27%)
  local copies, waits for them, and re-layouts  274 us (26%)
  waiting for transfers between devices  244 us (23%)
  matrix products  121 us (12%)
  other arithmetic  99.6 us (10%)
  between operations  13.7 us (1%)
    all_to_all x1, blocking collectives, body(): lax.all_to_all(proj_columns, 'my', split_axis=2, concat_axis=3, tiled=True)  214 us
    all_gather x1, waiting for transfers between devices, body(): lax.all_gather(grouped, 'my')  181 us
    all_gather x1, waiting for transfers between devices, body(): portion = lax.all_gather(gathered_rows, 'rep', axis=0, tiled=True)  62.8 us
    another operation x1, other arithmetic  61.7 us
    unnamed x4, local copies, waits for them, and re-layouts  50.6 us
    reshape x2, local copies, waits for them, and re-layouts, body(): jnp.concatenate(lax.all_gather(grouped, 'my'), axis=3)  43.8 us
    convert_element_type x1, other arithmetic, body(): noise_wide = noise_field.astype(jnp.float32)  37.8 us
    all_to_all x3, local copies, waits for them, and re-layouts, body(): lax.all_to_all(proj_columns, 'my', split_axis=2, concat_axis=3, tiled=True)  37.4 us
  transfers between devices with their start and end apart: 2, of which 2 were waited for; matrix products, arithmetic and copies ran while one was open for 4% of the time, Pallas kernels for 0%

profile of v1, /device:TPU:0, one launch (start us, length us, event | category | flops | bytes accessed | tf_op | source)
XLA Modules:
  0.0 1028.8 jit_solution(8334935528650138559)
XLA Ops:
  6.5 0.0 copy-start
  6.5 0.0 all-gather.3.cloned.1.call-start
  6.5 1.3 copy-done
  7.8 25.5 %convert_bitcast_fusion.3 = bf16[32,2,96,192]{2,0,3,1:T(8,128)(2,1)} fusion(bf16[2,192,96,384]{3,2,1,0:T(8,128)(2,1)} %param.3, bf16[384,1536]{1,0:T(8,128)(2,1)S(1)} %copy-done, s32[]{:T(128)S(6)} %select_n.10), kind=kOutput, calls=%fused_computation.17 | convolution fusion | flops 907149312 | bytes 30769156 | tf_op jit(solution)/shard_map/pabk,kz->zpba/dot_general | solution.py:28
  33.3 5.1 copy.47
  38.5 6.9 reshape.32
  45.3 31.8 %all_to_all.51 = bf16[32,2,18432]{2,1,0:T(2,128)(2,1)S(1)} all-to-all(bf16[32,2,18432]{2,1,0:T(2,128)(2,1)S(1)} %reshape.32), channel_id=1, replica_groups=mesh['rep'=4,'mx'=2,'my'=4] {'mx'}, dimensions={0} | all-to-all | bytes 4718592 | tf_op jit(solution)/shard_map/all_to_all | solution.py:32
  77.1 0.7 copy.54
  77.8 4.5 all_gather_reshape.3
  82.3 3.8 copy.28
  86.1 0.0 all-gather.3.cloned.1.call-update
  86.2 0.2 all-gather.5.cloned.1.call-start
  86.4 37.8 %convert_element_type.34 = f32[16,2,384,1536]{3,2,1,0:T(8,128)} convert(bf16[16,2,384,1536]{3,2,1,0:T(8,128)(2,1)} %param.4) | non-fusion elementwise | flops 18874368 | bytes 113246208 | tf_op jit(solution)/shard_map/convert_element_type | solution.py:48
  124.2 180.8 %all-gather.3.cloned.1.call-done = bf16[4,16,2,2,96,192]{5,4,3,2,1,0:T(8,128)(2,1)} async-done(((bf16[1,16,2,2,96,192]{5,4,3,2,1,0:T(8,128)(2,1)}), bf16[4,16,2,2,96,192]{5,4,3,2,1,0:T(8,128)(2,1)}) %all-gather.3.cloned.1.call-update) | async-done | bytes 9437200 | tf_op jit(solution)/shard_map/all_gather | solution.py:38
  305.0 23.7 %copy.29 = bf16[16,2,2,4,96,192]{4,3,5,2,1,0:T(4,128)(2,1)} copy(bf16[16,2,2,4,96,192]{5,4,2,1,0,3:T(8,128)(2,1)} %bitcast.92) | data formatting | bytes 18874368 | tf_op jit(solution)/shard_map/reshape | solution.py:38
  328.7 20.1 %reshape.21 = bf16[16,2,2,384,192]{3,4,2,1,0:T(8,128)(2,1)} reshape(bf16[16,2,2,4,96,192]{4,3,5,2,1,0:T(4,128)(2,1)} %copy.29) | data formatting | bytes 18874368 | tf_op jit(solution)/shard_map/reshape | solution.py:38
  348.8 10.7 %bitcast_convert_fusion.4 = bf16[16,2,384,384]{3,2,1,0:T(8,128)(2,1)} fusion(bf16[16,2,2,384,192]{3,4,2,1,0:T(8,128)(2,1)} %reshape.21, bf16[2,192,1536]{2,1,0:T(8,128)(2,1)S(1)} %bitcast.87, s32[]{:T(128)S(6)} %select_n.11), kind=kOutput, calls=%fused_computation.9.clone.clone.1 | convolution fusion | flops 3628597248 | bytes 19169284 | tf_op jit(solution)/shard_map/zpsal,slx->zpax/dot_general | solution.py:36
  359.5 34.1 %fusion.6 = f32[16,2,384,1536]{3,2,1,0:T(8,128)} fusion(bf16[384,1536]{1,0:T(8,128)(2,1)S(1)} %copy-done, bf16[16,2,384,384]{3,2,1,0:T(8,128)(2,1)} %bitcast_convert_fusion.4), kind=kOutput, calls=%fused_computation.10 | convolution fusion | flops 14495514624 | bytes 86114304 | tf_op jit(solution)/shard_map/zpax,ay->zpxy/dot_general | solution.py:42
  393.6 61.7 %fusion.1 = (bf16[16,1,384,1536]{3,2,1,0:T(8,128)(2,1)}, bf16[16,1,384,1536]{3,2,1,0:T(8,128)(2,1)}) fusion(f32[16,2,384,1536]{3,2,1,0:T(8,128)} %convert_element_type.34, f32[16,2,384,1536]{3,2,1,0:T(8,128)} %fusion.6), kind=kLoop, calls=%fused_computation.3 | loop fusion | flops 132120576 | bytes 188743680 | tf_op jit(solution)/shard_map/convert
  455.3 26.5 %convert_bitcast_fusion.1 = bf16[16,2,384,384]{2,3,1,0:T(8,128)(2,1)} fusion(bf16[16,1,384,1536]{3,2,1,0:T(8,128)(2,1)} %get-tuple-element.6, bf16[16,1,384,1536]{3,2,1,0:T(8,128)(2,1)} %get-tuple-element.5, bf16[384,1536]{1,0:T(8,128)(2,1)S(1)} %copy-done), kind=kOutput, calls=%fused_computation.14 | convolution fusion | flops 14519107584 | bytes 48365568 | tf_op jit(solution)/shard_map/zpxy,ny->zpnx/dot_general | solution.py:56
  481.9 23.9 %copy.31 = bf16[16,2,384,384]{3,1,0,2:T(2,128)(2,1)} copy(bf16[16,2,384,384]{2,3,1,0:T(8,128)(2,1)} %convert_bitcast_fusion.1) | data formatting | bytes 18874368 | tf_op jit(solution)/shard_map/convert_element_type | solution.py:58
  505.8 214.3 %all_to_all.52 = bf16[16,2,384,384]{3,1,0,2:T(2,128)(2,1)} all-to-all(bf16[16,2,384,384]{3,1,0,2:T(2,128)(2,1)} %copy.31), channel_id=1, replica_groups=mesh['rep'=4,'mx'=2,'my'=4] {'my'}, dimensions={2} | all-to-all | bytes 18874368 | tf_op jit(solution)/shard_map/all_to_all | solution.py:59
  720.1 10.9 %copy.32 = bf16[16,2,384,384]{3,2,1,0:T(8,128)(2,1)} copy(bf16[16,2,384,384]{3,1,0,2:T(2,128)(2,1)} %all_to_all.52) | data formatting | bytes 18874368 | tf_op jit(solution)/shard_map/all_to_all | solution.py:59
  731.0 10.6 %copy.33 = bf16[16,2,96,4,384]{4,3,2,1,0:T(4,128)(2,1)} copy(bf16[16,2,96,4,384]{4,2,3,1,0:T(8,128)(2,1)} %bitcast.91) | data formatting | bytes 18874368 | tf_op jit(solution)/shard_map/all_to_all | solution.py:59
  741.6 15.9 %reshape.29 = bf16[16,2,96,1536,1]{3,2,1,0,4:T(8,128)(2,1)} reshape(bf16[16,2,96,4,384]{4,3,2,1,0:T(4,128)(2,1)} %copy.33) | data formatting | bytes 18874368 | tf_op jit(solution)/shard_map/all_to_all | solution.py:59
  757.5 10.2 convert_bitcast_fusion.2
  767.6 35.2 %copy.48 = bf16[16,2,2,96,192]{0,1,4,3,2:T(2,128)(2,1)} copy(bf16[16,2,2,96,192]{4,3,2,1,0:T(8,128)(2,1)} %convert_bitcast_fusion.2) | data formatting | bytes 4718592 | tf_op jit(solution)/shard_map/reshape | solution.py:63
  802.9 27.0 %reshape.34 = bf16[2,2,294912]{2,1,0:T(2,128)(2,1)S(1)} reshape(bf16[36864,2,16]{2,1,0:T(2,128)(2,1)} %bitcast.88) | data formatting | bytes 4718592
  829.8 30.9 %all_to_all.53 = bf16[2,2,294912]{2,1,0:T(2,128)(2,1)} all-to-all(bf16[2,2,294912]{2,1,0:T(2,128)(2,1)S(1)} %reshape.34), channel_id=1, replica_groups=mesh['rep'=4,'mx'=2,'my'=4] {'mx'}, dimensions={0} | all-to-all | bytes 4718592 | tf_op jit(solution)/shard_map/all_to_all | solution.py:66
  860.7 22.4 %reshape.35 = bf16[36864,2,16]{2,1,0:T(2,128)(2,1)} reshape(bf16[2,2,294912]{2,1,0:T(2,128)(2,1)} %all_to_all.53) | data formatting | bytes 4718592
  883.1 35.6 %copy.36 = bf16[2,16,2,18432]{3,1,0,2:T(8,128)(2,1)} copy(bf16[2,16,2,18432]{1,2,3,0:T(2,128)(2,1)} %bitcast.89) | data formatting | bytes 4718592 | tf_op jit(solution)/shard_map/all_to_all | solution.py:66
  918.7 0.0 all-gather.5.cloned.1.call-update
  918.7 62.8 %all-gather.5.cloned.1.call-done = bf16[128,2,18432]{2,0,1:T(8,128)(2,1)} async-done(((bf16[32,2,18432]{2,0,1:T(8,128)(2,1)}), bf16[128,2,18432]{2,0,1:T(8,128)(2,1)}) %all-gather.5.cloned.1.call-update) | async-done | bytes 9437200 | tf_op jit(solution)/shard_map/all_gather | solution.py:70
  981.5 12.6 %copy.37 = bf16[128,2,18432]{0,2,1:T(8,128)(2,1)} copy(bf16[128,2,18432]{2,0,1:T(8,128)(2,1)} %all-gather.5.cloned.1.call-done) | data formatting | bytes 18874368 | tf_op jit(solution)/shard_map/all_gather | solution.py:70
  994.1 13.8 %convert_bitcast_fusion = bf16[2,192,96,96]{1,3,2,0:T(8,128)(2,1)} fusion(bf16[128,2,96,192]{0,3,2,1:T(8,128)(2,1)} %bitcast.90, bf16[384,1536]{1,0:T(8,128)(2,1)S(1)} %copy-done, s32[]{:T(128)S(6)} %select_n.9, s32[]{:T(128)S(6)} %add.30), kind=kOutput, calls=%fused_computation.13 | convolution fusion | flops 909508608 | bytes 16539656 | tf_op jit(solution)/shard_map/zpba,nz->pabn/dot_general | solution.py:72
  1007.9 13.9 %copy.38 = bf16[2,192,96,96]{3,2,1,0:T(8,128)(2,1)} copy(bf16[2,192,96,96]{1,3,2,0:T(8,128)(2,1)} %convert_bitcast_fusion) | data formatting | bytes 14155776 | tf_op jit(solution)/shard_map/convert_element_type | solution.py:73
Async XLA Ops:
  6.5 1.3 copy-start
  6.5 298.5 %all-gather.3.cloned.1.call-start = ((), (), s32[]{:S(2)}) async-start(), calls=%async_computation.3 | async-start | bytes 15728640 | tf_op jit(solution)/shard_map/all_gather | solution.py:38
  86.2 895.4 %all-gather.5.cloned.1.call-start = ((), (), s32[]{:S(2)}) async-start(), calls=%async_computation.4 | async-start | bytes 11796480 | tf_op jit(solution)/shard_map/all_gather | solution.py:70
Sparse Core Ops, SparseCore 0:
  86.3 218.6 all-gather.2
  918.8 62.6 all-gather.4
